TPU v7x, 32 devices: a 4x4x1 block of a 4x4x8 slice. The times are simulated.
32 devices in a mesh: ens: 1 (over z), col: 4 (over y), row: 8 (over x, core).
Axes of the slice: x: 4, y: 4, z: 1, core: 2. Of those that a mesh axis runs over, the one named last changes fastest.
The devices are a block of a 4x4x8 slice.
Arguments:
- u_init: float32 [2048, 2048], P(('ens', 'row'), 'col')
- v_init: float32 [2048, 2048], P(('ens', 'row'), 'col')
- stencil_w: float32 [64, 3, 3], replicated
Outputs:
- output 1: float32 [2048, 2048], P(('ens', 'row'), 'col')
- output 2: float32 [2048, 2048], P(('ens', 'row'), 'col')
All inputs are finite; a program needn't handle non-finite values.
Results may differ from a plain program's by a relative error of at most 0.001.
Values are sent between devices in bfloat16 or wider.
A program may use at most 768 MiB of HBM per device.

v0:
```python
import jax
import jax.numpy as jnp
from jax import lax
from jax.sharding import PartitionSpec as P

TIME_STEP = 0.5


def stencil_valid(block, step_w):
    out_rows = block.shape[0] - 2
    out_cols = block.shape[1] - 2
    total_acc = step_w[0, 0] * block[0:out_rows, 0:out_cols]
    for tap_index in range(1, 9):
        row_off, col_off = divmod(tap_index, 3)
        total_acc = total_acc + step_w[row_off, col_off] * block[row_off:row_off + out_rows, col_off:col_off + out_cols]
    return total_acc


def solution(mesh):
    row_devices = mesh.shape["row"]
    col_devices = mesh.shape["col"]
    row_fwd = [(source_dev, (source_dev + 1) % row_devices) for source_dev in range(row_devices)]
    row_back = [(source_dev, (source_dev - 1) % row_devices) for source_dev in range(row_devices)]
    col_fwd = [(source_dev, (source_dev + 1) % col_devices) for source_dev in range(col_devices)]
    col_back = [(source_dev, (source_dev - 1) % col_devices) for source_dev in range(col_devices)]
    tile_spec = P(("ens", "row"), "col")

    def halo_pad(u_tile):
        from_above = lax.ppermute(u_tile[-1:, :], "row", row_fwd)
        from_below = lax.ppermute(u_tile[:1, :], "row", row_back)
        tall_tile = jnp.concatenate([from_above, u_tile, from_below], axis=0)
        from_left = lax.ppermute(tall_tile[:, -1:], "col", col_fwd)
        from_right = lax.ppermute(tall_tile[:, :1], "col", col_back)
        return jnp.concatenate([from_left, tall_tile, from_right], axis=1)

    def local_run(u_tile, v_tile, stencil_w):
        def one_step(state_pair, step_w):
            u_now, v_now = state_pair
            padded = halo_pad(u_now)
            v_next = v_now + (stencil_valid(padded, step_w) - u_now)
            u_next = u_now + TIME_STEP * v_next
            return (u_next, v_next), None

        (u_final, v_final), _ = lax.scan(one_step, (u_tile, v_tile), stencil_w)
        return u_final, v_final

    return jax.shard_map(local_run, mesh=mesh, in_specs=(tile_spec, tile_spec, P()), out_specs=(tile_spec, tile_spec), check_vma=False)
```

profile of v0, /device:TPU:97, one launch (start us, length us, event | category | flops | bytes accessed | tf_op | source)
XLA Modules:
  0.0 1156.1 jit_solution(2154828256230059775)
XLA Ops:
  1.8 1153.2 %while.12 = (s32[]{:T(128)}, f32[256,512]{1,0:T(8,128)S(1)}, f32[256,512]{1,0:T(8,128)S(1)}, f32[64,3,3]{2,1,0:T(4,128)S(1)}, s32[]{:T(128)}) while((s32[]{:T(128)}, f32[256,512]{1,0:T(8,128)S(1)}, f32[256,512]{1,0:T(8,128)S(1)}, f32[64,3,3]{2,1,0:T(4,128)S(1)}, s32[]{:T(128)}) %tuple.49), condition=%wide.region_1.2_spmd, body=%wide.region_0.1_spmd.sunk | while | flops 3809814 | bytes 8448517 | solution.py:44
  14.0 6.4 multiply_add_fusion.2
  32.1 6.4 multiply_add_fusion.2
  50.2 6.4 multiply_add_fusion.2
  68.2 6.4 multiply_add_fusion.2
  86.2 6.4 multiply_add_fusion.2
  104.3 6.4 multiply_add_fusion.2
  122.1 6.4 multiply_add_fusion.2
  140.2 6.4 multiply_add_fusion.2
  158.3 6.4 multiply_add_fusion.2
  176.3 6.4 multiply_add_fusion.2
  194.2 6.4 multiply_add_fusion.2
  212.3 6.4 multiply_add_fusion.2
  230.3 6.4 multiply_add_fusion.2
  248.4 6.4 multiply_add_fusion.2
  266.2 6.4 multiply_add_fusion.2
  284.3 6.4 multiply_add_fusion.2
  302.3 6.4 multiply_add_fusion.2
  320.4 6.4 multiply_add_fusion.2
  338.3 6.4 multiply_add_fusion.2
  356.3 6.4 multiply_add_fusion.2
  374.4 6.4 multiply_add_fusion.2
  410.3 6.4 multiply_add_fusion.2
  428.4 6.4 multiply_add_fusion.2
  (948 shorter events, 1005.3 us)
Async XLA Ops:
  6.8 6.9 collective-permute-start.2
  26.2 5.6 collective-permute-start.2
  44.3 5.6 collective-permute-start.2
  74.7 5.6 collective-permute-start
  116.3 5.6 collective-permute-start.2
  146.7 5.7 collective-permute-start
  188.3 5.6 collective-permute-start.2
  218.7 5.7 collective-permute-start
  260.4 5.6 collective-permute-start.2
  290.8 5.7 collective-permute-start
  332.4 5.6 collective-permute-start.2
  362.8 5.7 collective-permute-start
  434.8 5.7 collective-permute-start
  506.9 5.7 collective-permute-start
  578.9 5.7 collective-permute-start
  650.9 5.7 collective-permute-start
  723.0 5.7 collective-permute-start
  795.0 5.7 collective-permute-start
  867.0 5.7 collective-permute-start
  908.7 5.6 collective-permute-start.2
  939.1 5.7 collective-permute-start
  980.7 5.6 collective-permute-start.2
  1011.1 5.7 collective-permute-start
  1083.1 5.7 collective-permute-start
  (237 other events, 903.0 us)
where the time goes:
time: 1160 us
  starting transfers between devices  484 us (42%)
  other arithmetic  434 us (37%)
  waiting for transfers between devices  186 us (16%)
  local copies, waits for them, and re-layouts  48.2 us (4%)
    add x64, other arithmetic, one_step(): u_next = u_now + TIME_STEP * v_next  409 us
    ppermute x64, starting transfers between devices, halo_pad(): from_below = lax.ppermute(u_tile[:1, :], 'row', row_back)  290 us
    ppermute x64, starting transfers between devices, halo_pad(): from_right = lax.ppermute(tall_tile[:, :1], 'col', col_back)  117 us
    ppermute x64, waiting for transfers between devices, halo_pad(): from_left = lax.ppermute(tall_tile[:, -1:], 'col', col_fwd)  107 us
    ppermute x64, starting transfers between devices, halo_pad(): from_left = lax.ppermute(tall_tile[:, -1:], 'col', col_fwd)  75.7 us
    ppermute x64, waiting for transfers between devices, halo_pad(): from_below = lax.ppermute(u_tile[:1, :], 'row', row_back)  52.6 us
    slice x64, local copies, waits for them, and re-layouts, stencil_valid(): total_acc = step_w[0, 0] * block[0:out_rows, 0:out_cols]  43.4 us
  transfers between devices with their start and end apart: 256, of which 208 were waited for; matrix products, arithmetic and copies ran while one was open for 4% of the time, Pallas kernels for 0%

commit v1 on v0

v1 whole, which is shorter than its diff:
```python
import functools

import jax
import jax.numpy as jnp
from jax import lax
from jax.experimental import pallas as pl
from jax.experimental.pallas import tpu as pltpu
from jax.sharding import PartitionSpec as P

LANES = 128
SUB = 8
NC = 5
MESH = pl.DeviceIdType.MESH


def lane_iota():
    return lax.broadcasted_iota(jnp.int32, (SUB, LANES), 1)


def permute(x, idx):
    return jnp.take_along_axis(x, idx, axis=1, mode="promise_in_bounds")


def pick(masks, parts):
    out = parts[0]
    for m, p in zip(masks[1:], parts[1:]):
        out = jnp.where(m, p, out)
    return out


def step_coeffs(w_ref, t):
    w = [[jnp.full((SUB, LANES), w_ref[a, b, t]) for b in range(3)] for a in range(2)]
    return (
        0.5 * w[0][1],
        0.5 * w[1][0],
        0.25 * (w[0][0] + w[0][2]),
        0.25 * (w[0][0] - w[0][2]),
        1.5 + 0.5 * w[1][1],
    )


def stencil_group(cur, prv, coeffs, r0):
    w01, w10, al, be, cc = coeffs
    above = cur[:, pl.ds(r0 - 1, SUB), :]
    mid = cur[:, pl.ds(r0, SUB), :]
    below = cur[:, pl.ds(r0 + 1, SUB), :]
    s = above + below
    q = al * s + w10 * mid
    r = be * (above - below)
    x = q + r
    y = q - r
    z = (w01 * s + cc * mid) - prv[:, pl.ds(r0, SUB), :]
    x_wrap = pltpu.roll(x[NC - 1], 1, 1)
    y_wrap = pltpu.roll(y[0], LANES - 1, 1)
    for c in range(NC):
        xc = x[c - 1] if c else x_wrap
        yc = y[c + 1] if c < NC - 1 else y_wrap
        prv[c, pl.ds(r0, SUB), :] = (z[c] + xc) + yc


def exchange(
    rows, cols, kr, halo, row_n, col_n,
    u_ref, v_ref, ru, rv, h_l, h_r,
    edge, pk_l, pk_r, in_sem, send_sem, recv_sem,
):
    my_row, my_col = lax.axis_index("row"), lax.axis_index("col")
    up, down = lax.rem(my_row + row_n - 1, row_n), lax.rem(my_row + 1, row_n)
    left, right = lax.rem(my_col + col_n - 1, col_n), lax.rem(my_col + 1, col_n)
    loads = []
    for i, (ref, col) in enumerate(((u_ref, 0), (v_ref, 0), (u_ref, cols - LANES), (v_ref, cols - LANES))):
        loads.append(pltpu.make_async_copy(ref.at[:, pl.ds(col, LANES)], edge.at[i], in_sem.at[i]))
        loads[-1].start()
    barrier = pltpu.get_barrier_semaphore()
    around = [(r, c) for r in (up, my_row, down) for c in (left, my_col, right)]
    around = [d for i, d in enumerate(around) if i != 4]
    for r, c in around:
        pl.semaphore_signal(barrier, inc=1, device_id={"row": r, "col": c}, device_id_type=MESH)
    for c in loads:
        c.wait()
    low = lane_iota() < halo

    def pack(g, _):
        at = pl.ds(pl.multiple_of(SUB * g, SUB), SUB)
        pk_l[at, :] = jnp.where(low, edge[0, at, :], pltpu.roll(edge[1, at, :], halo, 1))
        pk_r[at, :] = jnp.where(low, pltpu.roll(edge[3, at, :], halo, 1), edge[2, at, :])
        return 0

    lax.fori_loop(0, rows // SUB, pack, 0, unroll=8)
    pl.semaphore_wait(barrier, len(around))
    sends = []

    def send(src, dst, r, c):
        i = len(sends)
        copy = pltpu.make_async_remote_copy(
            src_ref=src, dst_ref=dst, send_sem=send_sem.at[i], recv_sem=recv_sem.at[i],
            device_id={"row": r, "col": c}, device_id_type=MESH,
        )
        copy.start()
        sends.append(copy)

    own, top, bottom = pl.ds(kr, rows), pl.ds(0, kr), pl.ds(kr + rows, kr)
    send(pk_l, h_r.at[own], my_row, left)
    send(pk_r, h_l.at[own], my_row, right)
    for n, r in ((u_ref, ru), (v_ref, rv)):
        send(n.at[pl.ds(0, kr)], r.at[pl.ds(kr, kr)], up, my_col)
        send(n.at[pl.ds(rows - kr, kr)], r.at[pl.ds(0, kr)], down, my_col)
    send(pk_l.at[pl.ds(0, kr)], h_r.at[bottom], up, left)
    send(pk_l.at[pl.ds(rows - kr, kr)], h_r.at[top], down, left)
    send(pk_r.at[pl.ds(0, kr)], h_l.at[bottom], up, right)
    send(pk_r.at[pl.ds(rows - kr, kr)], h_l.at[top], down, right)
    for c in sends:
        c.wait()


def kernel(
    rows, cols, steps, kr, halo,
    u_ref, v_ref, w_ref, ru, rv, h_l, h_r, uo_ref, vo_ref,
    nu, nv, x0, x1, in_sem, out_sem,
):
    own = pl.ds(0, rows)
    loads = [
        pltpu.make_async_copy(u_ref, nu, in_sem.at[0]),
        pltpu.make_async_copy(v_ref, nv, in_sem.at[1]),
    ]
    for c in loads:
        c.start()
    for c in loads:
        c.wait()
    lane = lane_iota()
    low = lane < halo
    nblk = cols // LANES

    residue = lax.rem(lane, NC)
    masks = [residue == m for m in range(NC)]

    def to_lanes(nu, nv, at, row0):
        out_row = SUB + row0
        hl, hr = h_l[pl.ds(row0, SUB), :], h_r[pl.ds(row0, SUB), :]
        uh = jnp.where(low, hr, hl)
        vh = pltpu.roll(jnp.where(low, hl, hr), halo, 1)
        ub = [nu[at, b * LANES : (b + 1) * LANES] for b in range(nblk)] + [uh]
        vb = [nv[at, b * LANES : (b + 1) * LANES] for b in range(nblk)] + [vh]
        for c in range(NC):
            idx = (NC * lane + (c - halo) % LANES) & (LANES - 1)
            res = [(c - halo - LANES * b) % NC for b in range(nblk + 1)]
            sel = [masks[k] for k in res]
            ul = 0.25 * permute(pick(sel, ub), idx)
            vl = permute(pick(sel, vb), idx)
            x0[c, pl.ds(out_row, SUB), :] = ul
            x1[c, pl.ds(out_row, SUB), :] = ul - 0.125 * vl

    for g in range(kr // SUB):
        to_lanes(ru, rv, pl.ds(SUB * g, SUB), SUB * g)
    for g in range(rows // SUB):
        to_lanes(nu, nv, pl.ds(SUB * g, SUB), kr + SUB * g)
    for g in range(kr // SUB):
        to_lanes(ru, rv, pl.ds(kr + SUB * g, SUB), kr + rows + SUB * g)

    base = SUB + kr
    done = 0
    while done < steps:
        left_steps = steps - done
        count = min(SUB, left_steps)
        ext = -(-(left_steps - 1) // SUB) * SUB

        def two(i, _, done=done, ext=ext):
            for j, (a, b) in enumerate(((x0, x1), (x1, x0))):
                coeffs = step_coeffs(w_ref, done + 2 * i + j)
                for r0 in range(base - ext, base + rows + ext, SUB):
                    stencil_group(a, b, coeffs, r0)
            return 0

        lax.fori_loop(0, count // 2, two, 0)
        done += count

    inv = pow(NC, -1, LANES)
    for g in range(rows // SUB):
        at = pl.ds(base + SUB * g, SUB)
        to = pl.ds(SUB * g, SUB)
        uu, vv = [], []
        for c in range(NC):
            idx = (inv * (lane + (halo - c) % LANES)) & (LANES - 1)
            now, old = x0[c, at, :], x1[c, at, :]
            uu.append(permute(4.0 * now, idx))
            vv.append(permute(8.0 * (now - old), idx))
        for b in range(nblk):
            sel = [masks[(c - halo - LANES * b) % NC] for c in range(NC)]
            nu[to, b * LANES : (b + 1) * LANES] = pick(sel, uu)
            nv[to, b * LANES : (b + 1) * LANES] = pick(sel, vv)
    stores = [
        pltpu.make_async_copy(nu.at[own], uo_ref, out_sem.at[0]),
        pltpu.make_async_copy(nv.at[own], vo_ref, out_sem.at[1]),
    ]
    for c in stores:
        c.start()
    for c in stores:
        c.wait()


def solution(mesh):
    row_n, col_n = mesh.shape["row"], mesh.shape["col"]
    spec = P(("ens", "row"), "col")

    def local_run(u, v, w):
        rows, cols = u.shape
        steps = w.shape[0]
        kr = -(-steps // SUB) * SUB
        halo = (NC * LANES - cols) // 2
        tall = rows + 2 * kr
        f32 = jnp.float32
        any_space = pl.BlockSpec(memory_space=pl.ANY)
        vmem = pl.BlockSpec(memory_space=pltpu.VMEM)
        smem = pl.BlockSpec(memory_space=pltpu.SMEM)
        halos = pl.pallas_call(
            functools.partial(exchange, rows, cols, kr, halo, row_n, col_n),
            out_shape=[jax.ShapeDtypeStruct((2 * kr, cols), f32)] * 2
            + [jax.ShapeDtypeStruct((tall, LANES), f32)] * 2,
            in_specs=[any_space] * 2,
            out_specs=[vmem] * 4,
            scratch_shapes=[
                pltpu.VMEM((4, rows, LANES), f32),
                pltpu.VMEM((rows, LANES), f32),
                pltpu.VMEM((rows, LANES), f32),
                pltpu.SemaphoreType.DMA((4,)),
                pltpu.SemaphoreType.DMA((10,)),
                pltpu.SemaphoreType.DMA((10,)),
            ],
            compiler_params=pltpu.CompilerParams(collective_id=0, has_side_effects=True),
        )(u, v)
        out = jax.ShapeDtypeStruct(u.shape, f32)
        return pl.pallas_call(
            functools.partial(kernel, rows, cols, steps, kr, halo),
            out_shape=(out, out),
            in_specs=[any_space, any_space, smem] + [vmem] * 4,
            out_specs=(any_space, any_space),
            scratch_shapes=[
                pltpu.VMEM((rows, cols), f32),
                pltpu.VMEM((rows, cols), f32),
                pltpu.VMEM((NC, tall + 2 * SUB, LANES), f32),
                pltpu.VMEM((NC, tall + 2 * SUB, LANES), f32),
                pltpu.SemaphoreType.DMA((2,)),
                pltpu.SemaphoreType.DMA((2,)),
            ],
        )(u, v, jnp.transpose(w, (1, 2, 0)), *halos)

    return jax.shard_map(
        local_run, mesh=mesh, in_specs=(spec, spec, P()), out_specs=(spec, spec), check_vma=False
    )
```

time: 1160 us -> 50.5 us (0.04)
  starting transfers between devices: 484 us -> 0 us
  other arithmetic: 434 us -> 0 us
  waiting for transfers between devices: 186 us -> 0 us
  Pallas kernels: 0 us -> 49.7 us
  local copies, waits for them, and re-layouts: 48.2 us -> 0 us
    ppermute x256 -> x0, starting transfers between devices: 484 us -> none  [the longest x64 290 us: halo_pad(): from_below = lax.ppermute(u_tile[:1, :], 'row', row_back)]
    add x64 -> x0, other arithmetic: 409 us -> none  [one_step(): u_next = u_now + TIME_STEP * v_next]
    ppermute x256 -> x0, waiting for transfers between devices: 186 us -> none  [the longest x64 107 us: halo_pad(): from_left = lax.ppermute(tall_tile[:, -1:], 'col', col_fwd)]
    pallas_call x0 -> x2, Pallas kernels: none -> 49.7 us  [the longest x1 35.5 us: local_run(): pl.pallas_call(functools.partial(kernel, rows, cols, steps, kr, halo), ou...]
    slice x128 -> x0, local copies, waits for them, and re-layouts: 43.7 us -> none  [the longest x64 43.4 us: stencil_valid(): total_acc = step_w[0, 0] * block[0:out_rows, 0:out_cols]]
    concatenate x64 -> x0, other arithmetic: 18.2 us -> none  [halo_pad(): return jnp.concatenate([from_left, tall_tile, from_right], axis=1)]
  transfers between devices with their start and end apart: 256 -> 0, of which waited for: 208 -> 0; matrix products, arithmetic and copies ran while one was open for 4% -> 0% of each run, Pallas kernels for 0% -> 0%
where the time goes in v1:
time: 50.5 us; the launch traced here: 50.3 us
  Pallas kernels  49.7 us (98%)
  between operations  0.64 us (1%)
    pallas_call x1, Pallas kernels, local_run(): pl.pallas_call(functools.partial(kernel, rows, cols, steps, kr, halo), ou...  35.5 us
    pallas_call x1, Pallas kernels, local_run(): pl.pallas_call(functools.partial(exchange, rows, cols, kr, halo, row_n, c...  14.2 us

profile of v1, /device:TPU:97, one launch (start us, length us, event | category | flops | bytes accessed | tf_op | source)
XLA Modules:
  0.0 50.3 jit_solution(15454815553935688145)
XLA Ops:
  0.6 14.2 %shard_map.50 = (f32[128,512]{1,0:T(8,128)}, f32[128,512]{1,0:T(8,128)}, f32[384,128]{1,0:T(8,128)}, f32[384,128]{1,0:T(8,128)}) custom-call(f32[256,512]{1,0:T(8,128)} %u_ref.3, f32[256,512]{1,0:T(8,128)} %v_ref.3), custom_call_target="tpu_custom_call" | custom-call | tf_op jit(solution)/shard_map/pallas_call | solution.py:214
  14.8 35.5 %shard_map.51 = (f32[256,512]{1,0:T(8,128)}, f32[256,512]{1,0:T(8,128)}) custom-call(f32[256,512]{1,0:T(8,128)} %u_ref.3, f32[256,512]{1,0:T(8,128)} %v_ref.3, f32[3,3,64]{2,1,0:T(4,128)} %bitcast.1, f32[128,512]{1,0:T(8,128)} %get-tuple-element.6.ru, f32[128,512]{1,0:T(8,128)} %get-tuple-element.7.rv, f32[384,128]{1,0:T(8,128)} %get-tuple-element.8.h_l, ...), custom_call_target="tpu_custom_call" | custom-call | tf_op jit(solution)/shard_map/pallas_call | solution.py:231

commit v2 on v1

v2 whole, which is shorter than its diff:
```python
import functools

import jax
import jax.numpy as jnp
from jax import lax
from jax.experimental import pallas as pl
from jax.experimental.pallas import tpu as pltpu
from jax.sharding import PartitionSpec as P

LANES = 128
SUB = 8
NC = 5
PAD = 3 * SUB
MESH = pl.DeviceIdType.MESH


def lane_iota():
    return lax.broadcasted_iota(jnp.int32, (SUB, LANES), 1)


def permute(x, idx):
    return jnp.take_along_axis(x, idx, axis=1, mode="promise_in_bounds")


def pick(masks, parts):
    out = parts[0]
    for m, p in zip(masks[1:], parts[1:]):
        out = jnp.where(m, p, out)
    return out


def step_coeffs(w_ref, t):
    w = [[jnp.full((SUB, LANES), w_ref[a, b, t]) for b in range(3)] for a in range(2)]
    return (
        0.5 * w[0][1],
        0.5 * w[1][0],
        0.25 * (w[0][0] + w[0][2]),
        0.25 * (w[0][0] - w[0][2]),
        1.5 + 0.5 * w[1][1],
    )


def stencil_group(cur, prv, coeffs, r0):
    w01, w10, al, be, cc = coeffs
    above = cur[:, pl.ds(r0 - 1, SUB), :]
    mid = cur[:, pl.ds(r0, SUB), :]
    below = cur[:, pl.ds(r0 + 1, SUB), :]
    s = above + below
    q = al * s + w10 * mid
    r = be * (above - below)
    x = q + r
    y = q - r
    z = (w01 * s + cc * mid) - prv[:, pl.ds(r0, SUB), :]
    x_wrap = pltpu.roll(x[NC - 1], 1, 1)
    y_wrap = pltpu.roll(y[0], LANES - 1, 1)
    for c in range(NC):
        xc = x[c - 1] if c else x_wrap
        yc = y[c + 1] if c < NC - 1 else y_wrap
        prv[c, pl.ds(r0, SUB), :] = (z[c] + xc) + yc


def kernel(
    rows, cols, steps, kr, halo, row_n, col_n,
    u_ref, v_ref, w_ref, uo_ref, vo_ref,
    nu, nv, pk_l, pk_r, h_l, h_r, x0, x1, got,
    in_sem, out_sem, send_sem, recv_sem, edge_send, edge_recv,
):
    my_row, my_col = lax.axis_index("row"), lax.axis_index("col")
    up, down = lax.rem(my_row + row_n - 1, row_n), lax.rem(my_row + 1, row_n)
    left, right = lax.rem(my_col + col_n - 1, col_n), lax.rem(my_col + 1, col_n)
    own = pl.ds(kr, rows)
    loads = [
        pltpu.make_async_copy(u_ref, nu.at[own], in_sem.at[0]),
        pltpu.make_async_copy(v_ref, nv.at[own], in_sem.at[1]),
    ]
    for c in loads:
        c.start()
    barrier = pltpu.get_barrier_semaphore()
    around = [(r, c) for r in (up, my_row, down) for c in (left, my_col, right)]
    around = [d for i, d in enumerate(around) if i != 4]
    for r, c in around:
        pl.semaphore_signal(barrier, inc=1, device_id={"row": r, "col": c}, device_id_type=MESH)
    for c in loads:
        c.wait()
    lane = lane_iota()
    low = lane < halo
    nblk = cols // LANES

    def pack(g, _):
        src = pl.ds(pl.multiple_of(kr + SUB * g, SUB), SUB)
        dst = pl.ds(pl.multiple_of(SUB * g, SUB), SUB)
        u_first, v_first = nu[src, :LANES], nv[src, :LANES]
        u_last, v_last = nu[src, cols - LANES :], nv[src, cols - LANES :]
        pk_l[dst, :] = jnp.where(low, u_first, pltpu.roll(v_first, halo, 1))
        pk_r[dst, :] = jnp.where(low, pltpu.roll(v_last, halo, 1), u_last)
        return 0

    lax.fori_loop(0, rows // SUB, pack, 0, unroll=8)
    pl.semaphore_wait(barrier, len(around))
    sends = []

    def send(src, dst, r, c):
        i = len(sends)
        copy = pltpu.make_async_remote_copy(
            src_ref=src, dst_ref=dst, send_sem=send_sem.at[i], recv_sem=recv_sem.at[i],
            device_id={"row": r, "col": c}, device_id_type=MESH,
        )
        copy.start()
        sends.append(copy)

    top, bottom = pl.ds(0, kr), pl.ds(kr + rows, kr)
    send(pk_l, h_r.at[own], my_row, left)
    send(pk_r, h_l.at[own], my_row, right)
    for n in (nu, nv):
        send(n.at[pl.ds(kr, kr)], n.at[bottom], up, my_col)
        send(n.at[pl.ds(rows, kr)], n.at[top], down, my_col)
    send(pk_l.at[pl.ds(0, kr)], h_r.at[bottom], up, left)
    send(pk_l.at[pl.ds(rows - kr, kr)], h_r.at[top], down, left)
    send(pk_r.at[pl.ds(0, kr)], h_l.at[bottom], up, right)
    send(pk_r.at[pl.ds(rows - kr, kr)], h_l.at[top], down, right)
    for c in sends:
        c.wait()

    residue = lax.rem(lane, NC)
    masks = [residue == m for m in range(NC)]
    base = PAD

    def to_lanes(g, _):
        at = pl.ds(pl.multiple_of(SUB * g, SUB), SUB)
        out = pl.ds(pl.multiple_of(base - kr + SUB * g, SUB), SUB)
        hl, hr = h_l[at, :], h_r[at, :]
        uh = jnp.where(low, hr, hl)
        vh = pltpu.roll(jnp.where(low, hl, hr), halo, 1)
        ub = [nu[at, b * LANES : (b + 1) * LANES] for b in range(nblk)] + [uh]
        vb = [nv[at, b * LANES : (b + 1) * LANES] for b in range(nblk)] + [vh]
        for c in range(NC):
            idx = (NC * lane + (c - halo) % LANES) & (LANES - 1)
            sel = [masks[(c - halo - LANES * b) % NC] for b in range(nblk + 1)]
            ul = 0.25 * permute(pick(sel, ub), idx)
            vl = permute(pick(sel, vb), idx)
            x0[c, out, :] = ul
            x1[c, out, :] = ul - 0.125 * vl
        return 0

    lax.fori_loop(0, (rows + 2 * kr) // SUB, to_lanes, 0, unroll=4)

    par = lax.rem(my_row, 2)
    sign = 2 * par - 1
    cut = rows // 2
    n_big = (cut + kr) // SUB
    partners = (lax.rem(my_row + sign + row_n, row_n), lax.rem(my_row - sign + row_n, row_n))
    edge_at = ((rows - kr) * par, (rows - kr) * (1 - par))
    halo_at = ((rows + kr) * par - kr, rows - (rows + kr) * par)

    def edge_copies(half, p):
        slot = lax.rem(p, 2)
        src = pl.ds(pl.multiple_of(base + edge_at[half], SUB), kr)
        return [
            pltpu.make_async_remote_copy(
                src_ref=x.at[:, src, :], dst_ref=got.at[half, slot, i],
                send_sem=edge_send.at[half, slot, i], recv_sem=edge_recv.at[half, slot, i],
                device_id={"row": partners[half]}, device_id_type=MESH,
            )
            for i, x in enumerate((x0, x1))
        ]

    def half_steps(half, t_base, t0, count, n):
        start = (cut - SUB * n * (1 - par), cut - SUB * n * par)[half]

        def two(i, _):
            for j, (a, b) in enumerate(((x0, x1), (x1, x0))):
                t = t0 + 2 * i + j
                coeffs = step_coeffs(w_ref, t_base + t)
                r0 = base + start + sign * t
                for g in range(n):
                    stencil_group(a, b, coeffs, r0 + SUB * g)
            return 0

        lax.fori_loop(0, count // 2, two, 0)

    n_phase = steps // kr

    def phase(p, _):
        for half in range(2):
            @pl.when(p > 0)
            def _():
                for c in edge_copies(half, p - 1):
                    c.wait()
                slot = lax.rem(p - 1, 2)
                dst = pl.ds(pl.multiple_of(base + halo_at[half], SUB), kr)
                x0[:, dst, :] = got[half, slot, 0]
                x1[:, dst, :] = got[half, slot, 1]

            n_late = n_big - kr // SUB if half == 0 else n_big
            half_steps(half, kr * p, 0, kr // 2, n_big)
            half_steps(half, kr * p, kr // 2, kr // 2, n_late)

            @pl.when(p < n_phase - 1)
            def _():
                for c in edge_copies(half, p):
                    c.start()
        return 0

    lax.fori_loop(0, n_phase, phase, 0)

    inv = pow(NC, -1, LANES)

    def to_natural(g, _):
        at = pl.ds(pl.multiple_of(base + SUB * g, SUB), SUB)
        to = pl.ds(pl.multiple_of(kr + SUB * g, SUB), SUB)
        uu, vv = [], []
        for c in range(NC):
            idx = (inv * (lane + (halo - c) % LANES)) & (LANES - 1)
            now, old = x0[c, at, :], x1[c, at, :]
            uu.append(permute(4.0 * now, idx))
            vv.append(permute(8.0 * (now - old), idx))
        for b in range(nblk):
            sel = [masks[(c - halo - LANES * b) % NC] for c in range(NC)]
            nu[to, b * LANES : (b + 1) * LANES] = pick(sel, uu)
            nv[to, b * LANES : (b + 1) * LANES] = pick(sel, vv)
        return 0

    lax.fori_loop(0, rows // SUB, to_natural, 0, unroll=4)
    stores = [
        pltpu.make_async_copy(nu.at[own], uo_ref, out_sem.at[0]),
        pltpu.make_async_copy(nv.at[own], vo_ref, out_sem.at[1]),
    ]
    for c in stores:
        c.start()
    for c in stores:
        c.wait()


def solution(mesh):
    row_n, col_n = mesh.shape["row"], mesh.shape["col"]
    spec = P(("ens", "row"), "col")

    def local_run(u, v, w):
        rows, cols = u.shape
        steps = w.shape[0]
        kr = 2 * SUB
        halo = (NC * LANES - cols) // 2
        tall = rows + 2 * kr
        f32 = jnp.float32
        out = jax.ShapeDtypeStruct(u.shape, f32)
        return pl.pallas_call(
            functools.partial(kernel, rows, cols, steps, kr, halo, row_n, col_n),
            out_shape=(out, out),
            in_specs=[
                pl.BlockSpec(memory_space=pl.ANY),
                pl.BlockSpec(memory_space=pl.ANY),
                pl.BlockSpec(memory_space=pltpu.SMEM),
            ],
            out_specs=(pl.BlockSpec(memory_space=pl.ANY), pl.BlockSpec(memory_space=pl.ANY)),
            scratch_shapes=[
                pltpu.VMEM((tall, cols), f32),
                pltpu.VMEM((tall, cols), f32),
                pltpu.VMEM((rows, LANES), f32),
                pltpu.VMEM((rows, LANES), f32),
                pltpu.VMEM((tall, LANES), f32),
                pltpu.VMEM((tall, LANES), f32),
                pltpu.VMEM((NC, rows + 2 * PAD, LANES), f32),
                pltpu.VMEM((NC, rows + 2 * PAD, LANES), f32),
                pltpu.VMEM((2, 2, 2, NC, kr, LANES), f32),
                pltpu.SemaphoreType.DMA((2,)),
                pltpu.SemaphoreType.DMA((2,)),
                pltpu.SemaphoreType.DMA((10,)),
                pltpu.SemaphoreType.DMA((10,)),
                pltpu.SemaphoreType.DMA((2, 2, 2)),
                pltpu.SemaphoreType.DMA((2, 2, 2)),
            ],
            compiler_params=pltpu.CompilerParams(collective_id=0, has_side_effects=True),
        )(u, v, jnp.transpose(w, (1, 2, 0)))

    return jax.shard_map(
        local_run, mesh=mesh, in_specs=(spec, spec, P()), out_specs=(spec, spec), check_vma=False
    )
```

time: 50.5 us -> 49.6 us (0.982)
  Pallas kernels: 49.7 us -> 46.1 us
  local copies, waits for them, and re-layouts: 0 us -> 2.72 us
    pallas_call x2 -> x1, Pallas kernels: 49.7 us -> 46.1 us  [local_run(): pl.pallas_call(functools.partial(kernel, rows, cols, steps, kr, halo, row...]
    unnamed x0 -> x4, local copies, waits for them, and re-layouts: none -> 2.72 us
where the time goes in v2:
time: 49.6 us; the launch traced here: 49.5 us
  Pallas kernels  46.1 us (93%)
  local copies, waits for them, and re-layouts  2.72 us (5%)
  between operations  0.65 us (1%)
    pallas_call x1, Pallas kernels, local_run(): pl.pallas_call(functools.partial(kernel, rows, cols, steps, kr, halo, row...  46.1 us
    unnamed x4, local copies, waits for them, and re-layouts  2.72 us

profile of v2, /device:TPU:97, one launch (start us, length us, event | category | flops | bytes accessed | tf_op | source)
XLA Modules:
  0.0 49.5 jit_solution(14248444968893595224)
XLA Ops:
  0.6 46.1 %shard_map.50 = (f32[256,512]{1,0:T(8,128)}, f32[256,512]{1,0:T(8,128)}) custom-call(f32[256,512]{1,0:T(8,128)} %u_ref.1, f32[256,512]{1,0:T(8,128)} %v_ref.1, f32[3,3,64]{2,1,0:T(4,128)} %bitcast.1), custom_call_target="tpu_custom_call" | custom-call | tf_op jit(solution)/shard_map/pallas_call | solution.py:246
  46.7 0.0 copy-start
  46.7 1.9 %copy.7 = f32[256,512]{1,0:T(8,128)} copy(f32[256,512]{1,0:T(8,128)} %get-tuple-element.4) | data formatting | bytes 1048576
  48.7 0.0 copy-done
  48.7 0.8 %copy.8 = f32[256,512]{1,0:T(8,128)} copy(f32[256,512]{1,0:T(8,128)S(1)} %copy-done) | data formatting | bytes 1048576
Async XLA Ops:
  46.7 1.9 %copy-start = (f32[256,512]{1,0:T(8,128)S(1)}, f32[256,512]{1,0:T(8,128)}, u32[]{:S(2)}) copy-start(f32[256,512]{1,0:T(8,128)} %get-tuple-element.5) | copy-start | bytes 1572868

commit v3 on v2

v3 whole, which is shorter than its diff:
```python
import functools

import jax
import jax.numpy as jnp
from jax import lax
from jax.experimental import pallas as pl
from jax.experimental.pallas import tpu as pltpu
from jax.sharding import PartitionSpec as P

LANES = 128
SUB = 8
NC = 5
UNROLL = 4
FIRST = 10
PAD = 3 * SUB
MESH = pl.DeviceIdType.MESH


def lane_iota():
    return lax.broadcasted_iota(jnp.int32, (SUB, LANES), 1)


def permute(x, idx):
    return lax.gather(
        x, idx[..., None],
        lax.GatherDimensionNumbers(
            offset_dims=(), collapsed_slice_dims=(1,), start_index_map=(1,),
            operand_batching_dims=(0,), start_indices_batching_dims=(0,),
        ),
        slice_sizes=(1, 1), mode=lax.GatherScatterMode.PROMISE_IN_BOUNDS,
    )


def pick(masks, parts):
    out = parts[0]
    for m, p in zip(masks[1:], parts[1:]):
        out = jnp.where(m, p, out)
    return out


def step_coeffs(w_ref, t):
    w = [[jnp.full((SUB, LANES), w_ref[a, b, t]) for b in range(3)] for a in range(2)]
    return (
        0.5 * w[0][1],
        0.5 * w[1][0],
        0.25 * (w[0][0] + w[0][2]),
        0.25 * (w[0][0] - w[0][2]),
        1.5 + 0.5 * w[1][1],
    )


def stencil_group(xs, cur, coeffs, r0):
    w01, w10, al, be, cc = coeffs
    prv = 1 - cur
    above = xs[cur, :, pl.ds(r0 - 1, SUB), :]
    mid = xs[cur, :, pl.ds(r0, SUB), :]
    below = xs[cur, :, pl.ds(r0 + 1, SUB), :]
    s = above + below
    q = al * s + w10 * mid
    r = be * (above - below)
    x = q + r
    y = q - r
    z = (w01 * s + cc * mid) - xs[prv, :, pl.ds(r0, SUB), :]
    x_wrap = pltpu.roll(x[NC - 1], 1, 1)
    y_wrap = pltpu.roll(y[0], LANES - 1, 1)
    for c in range(NC):
        xc = x[c - 1] if c else x_wrap
        yc = y[c + 1] if c < NC - 1 else y_wrap
        xs[prv, c, pl.ds(r0, SUB), :] = (z[c] + xc) + yc


def kernel(
    rows, cols, steps, kr, halo, row_n, col_n,
    u_ref, v_ref, w_hbm, now_ref, old_ref,
    w_ref, table, nu, nv, pk_l, pk_r, h_l, h_r, xs, got,
    near, in_sem, send_sem, recv_sem, edge_send, edge_recv,
):
    my_row, my_col = lax.axis_index("row"), lax.axis_index("col")
    up, down = lax.rem(my_row + row_n - 1, row_n), lax.rem(my_row + 1, row_n)
    left, right = lax.rem(my_col + col_n - 1, col_n), lax.rem(my_col + 1, col_n)
    own = pl.ds(kr, rows)
    loads = [
        pltpu.make_async_copy(u_ref, nu.at[own], in_sem.at[0]),
        pltpu.make_async_copy(v_ref, nv.at[own], in_sem.at[1]),
    ]
    load_w = pltpu.make_async_copy(w_hbm, w_ref, in_sem.at[2])
    for c in (*loads, load_w):
        c.start()
    barrier = pltpu.get_barrier_semaphore()
    around = [(my_row, left), (my_row, right), (up, my_col), (down, my_col)]
    for r, c in around:
        pl.semaphore_signal(barrier, inc=1, device_id={"row": r, "col": c}, device_id_type=MESH)
    for c in loads:
        c.wait()
    x0, x1 = xs.at[0], xs.at[1]
    lane = lane_iota()
    low = lane < halo
    nblk = cols // LANES

    def pack(g, _):
        src = pl.ds(pl.multiple_of(kr + SUB * g, SUB), SUB)
        dst = pl.ds(pl.multiple_of(SUB * g, SUB), SUB)
        u_first, v_first = nu[src, :LANES], nv[src, :LANES]
        u_last, v_last = nu[src, cols - LANES :], nv[src, cols - LANES :]
        pk_l[dst, :] = jnp.where(low, u_first, pltpu.roll(v_first, halo, 1))
        pk_r[dst, :] = jnp.where(low, pltpu.roll(v_last, halo, 1), u_last)
        return 0

    lax.fori_loop(0, rows // SUB, pack, 0, unroll=8)
    pl.semaphore_wait(barrier, len(around))
    sends = []

    def send(src, dst, r, c):
        i = len(sends)
        copy = pltpu.make_async_remote_copy(
            src_ref=src, dst_ref=dst, send_sem=send_sem.at[i], recv_sem=recv_sem.at[i],
            device_id={"row": r, "col": c}, device_id_type=MESH,
        )
        copy.start()
        sends.append(copy)

    top, bottom = pl.ds(0, kr), pl.ds(kr + rows, kr)
    half = rows // 2
    for first in (0, half):
        at = pl.ds(first, half)
        to = pl.ds(kr + first, half)
        send(pk_l.at[at], h_r.at[to], my_row, left)
        send(pk_r.at[at], h_l.at[to], my_row, right)
        if first:
            break
        for n in (nu, nv):
            send(n.at[pl.ds(kr, kr)], n.at[bottom], up, my_col)
            send(n.at[pl.ds(rows, kr)], n.at[top], down, my_col)
        for r in (up, down):
            pl.semaphore_signal(near, inc=1, device_id={"row": r}, device_id_type=MESH)
        pl.semaphore_wait(near, 2)
        send(pk_l.at[pl.ds(0, kr)], h_r.at[bottom], up, left)
        send(pk_l.at[pl.ds(rows - kr, kr)], h_r.at[top], down, left)
        send(pk_r.at[pl.ds(0, kr)], h_l.at[bottom], up, right)
        send(pk_r.at[pl.ds(rows - kr, kr)], h_l.at[top], down, right)
    residue = lax.rem(lane, NC)
    masks = [residue == m for m in range(NC)]
    base = PAD
    load_w.wait()

    def tabulate(t, _):
        for k, x in enumerate(step_coeffs(w_ref, t)):
            table[t, k] = x
        return 0

    lax.fori_loop(0, steps, tabulate, 0, unroll=4)
    for c in sends:
        c.wait()

    def unpack(g, _):
        at = pl.ds(pl.multiple_of(SUB * g, SUB), SUB)
        hl, hr = h_l[at, :], h_r[at, :]
        h_l[at, :] = jnp.where(low, hr, hl)
        h_r[at, :] = pltpu.roll(jnp.where(low, hl, hr), halo, 1)
        return 0

    groups = (rows + 2 * kr) // SUB
    lax.fori_loop(0, groups, unpack, 0, unroll=groups // 3)

    for c in range(NC):
        idx = (NC * lane + (c - halo) % LANES) & (LANES - 1)
        sel = [masks[(c - halo - LANES * b) % NC] for b in range(nblk + 1)]

        def to_lanes(g, _, c=c, idx=idx, sel=sel):
            at = pl.ds(pl.multiple_of(SUB * g, SUB), SUB)
            out = pl.ds(pl.multiple_of(base - kr + SUB * g, SUB), SUB)
            ub = [nu[at, b * LANES : (b + 1) * LANES] for b in range(nblk)] + [h_l[at, :]]
            vb = [nv[at, b * LANES : (b + 1) * LANES] for b in range(nblk)] + [h_r[at, :]]
            ul = 0.25 * permute(pick(sel, ub), idx)
            vl = permute(pick(sel, vb), idx)
            x0[c, out, :] = ul
            x1[c, out, :] = ul - 0.125 * vl
            return 0

        lax.fori_loop(0, groups, to_lanes, 0, unroll=groups // 3)

    TOP, BOTTOM = 0, 1
    cut = SUB * FIRST
    part = lax.rem(my_row, 2)
    many, fewer, other = FIRST + kr // SUB, FIRST, (rows - cut + kr) // SUB
    mid = kr // 2
    n_phase = steps // kr

    def edge_copies(side, slot):
        src = pl.ds(base + (0, rows - kr)[side], kr)
        return [
            pltpu.make_async_remote_copy(
                src_ref=x.at[:, src, :], dst_ref=got.at[1 - side, slot, i],
                send_sem=edge_send.at[side, slot, i], recv_sem=edge_recv.at[1 - side, slot, i],
                device_id={"row": (up, down)[side]}, device_id_type=MESH,
            )
            for i, x in enumerate((x0, x1))
        ]

    def take_halo(side, p):
        @pl.when(p > 0)
        def _():
            slot = lax.rem(p - 1, 2)
            for c in edge_copies(side, slot):
                c.wait_send()
            for c in edge_copies(1 - side, slot):
                c.wait_recv()
            dst = pl.ds(base + (-kr, rows)[side], kr)
            x0[:, dst, :] = got[side, slot, 0]
            x1[:, dst, :] = got[side, slot, 1]

    def send_edge(side, p):
        @pl.when(p < n_phase - 1)
        def _():
            for c in edge_copies(side, lax.rem(p, 2)):
                c.start()

    def part_steps(p, t0, count, start, sign, n):
        def some(i, _):
            for j in range(UNROLL):
                t = kr * p + t0 + UNROLL * i + j
                coeffs = [table[t, k] for k in range(5)]
                r0 = base + start + sign * (t0 + j) + sign * UNROLL * i
                for g in range(n):
                    stencil_group(xs, j % 2, coeffs, r0 + SUB * g)
            return 0

        lax.fori_loop(0, count // UNROLL, some, 0)

    def phase(p, _):
        @pl.when(part == 0)
        def _():
            take_halo(TOP, p)
            part_steps(p, 0, mid, cut - SUB * many, -1, many)
            part_steps(p, mid, kr - mid, cut - SUB * fewer, -1, fewer)
            send_edge(TOP, p)
            take_halo(BOTTOM, p)
            part_steps(p, 0, kr, cut, -1, other)
            send_edge(BOTTOM, p)

        @pl.when(part == 1)
        def _():
            take_halo(BOTTOM, p)
            part_steps(p, 0, mid, rows - cut, 1, many)
            part_steps(p, mid, kr - mid, rows - cut, 1, fewer)
            send_edge(BOTTOM, p)
            take_halo(TOP, p)
            part_steps(p, 0, kr, rows - cut - SUB * other, 1, other)
            send_edge(TOP, p)

        return 0

    lax.fori_loop(0, n_phase, phase, 0)

    inv = pow(NC, -1, LANES)
    idx = [(inv * (lane + (halo - c) % LANES)) & (LANES - 1) for c in range(NC)]

    def to_natural(g, _):
        at = pl.ds(pl.multiple_of(base + SUB * g, SUB), SUB)
        to = pl.ds(pl.multiple_of(SUB * g, SUB), SUB)
        for x, out in ((x0, now_ref), (x1, old_ref)):
            parts = [permute(x[c, at, :], idx[c]) for c in range(NC)]
            for b in range(nblk):
                sel = [masks[(c - halo - LANES * b) % NC] for c in range(NC)]
                out[to, b * LANES : (b + 1) * LANES] = pick(sel, parts)
        return 0

    lax.fori_loop(0, rows // SUB, to_natural, 0, unroll=8)


def solution(mesh):
    row_n, col_n = mesh.shape["row"], mesh.shape["col"]
    spec = P(("ens", "row"), "col")

    def local_run(u, v, w):
        rows, cols = u.shape
        steps = w.shape[0]
        kr = 2 * SUB
        halo = (NC * LANES - cols) // 2
        tall = rows + 2 * kr
        f32 = jnp.float32
        out = jax.ShapeDtypeStruct(u.shape, f32)
        now, old = pl.pallas_call(
            functools.partial(kernel, rows, cols, steps, kr, halo, row_n, col_n),
            out_shape=(out, out),
            in_specs=[
                pl.BlockSpec(memory_space=pl.ANY),
                pl.BlockSpec(memory_space=pl.ANY),
                pl.BlockSpec(memory_space=pl.ANY),
            ],
            out_specs=(pl.BlockSpec(memory_space=pltpu.VMEM), pl.BlockSpec(memory_space=pltpu.VMEM)),
            scratch_shapes=[
                pltpu.SMEM((3, 3, steps), f32),
                pltpu.VMEM((steps, 5, SUB, LANES), f32),
                pltpu.VMEM((tall, cols), f32),
                pltpu.VMEM((tall, cols), f32),
                pltpu.VMEM((rows, LANES), f32),
                pltpu.VMEM((rows, LANES), f32),
                pltpu.VMEM((tall, LANES), f32),
                pltpu.VMEM((tall, LANES), f32),
                pltpu.VMEM((2, NC, rows + 2 * PAD, LANES), f32),
                pltpu.VMEM((2, 2, 2, NC, kr, LANES), f32),
                pltpu.SemaphoreType.REGULAR,
                pltpu.SemaphoreType.DMA((3,)),
                pltpu.SemaphoreType.DMA((12,)),
                pltpu.SemaphoreType.DMA((12,)),
                pltpu.SemaphoreType.DMA((2, 2, 2)),
                pltpu.SemaphoreType.DMA((2, 2, 2)),
            ],
            compiler_params=pltpu.CompilerParams(collective_id=0, has_side_effects=True),
        )(u, v, jnp.transpose(w, (1, 2, 0)))
        return 4.0 * now, 8.0 * (now - old)

    return jax.shard_map(
        local_run, mesh=mesh, in_specs=(spec, spec, P()), out_specs=(spec, spec), check_vma=False
    )
```

time: 49.6 us -> 43.3 us (0.87)
  Pallas kernels: 46.1 us -> 40.3 us
  local copies, waits for them, and re-layouts: 2.72 us -> 0 us
  other arithmetic: 0 us -> 2.3 us
    pallas_call x1, Pallas kernels: 46.1 us -> 40.3 us  [local_run(): pl.pallas_call(functools.partial(kernel, rows, cols, steps, kr, halo, row...]
    unnamed x4 -> x0, local copies, waits for them, and re-layouts: 2.72 us -> none
    mul x0 -> x1, other arithmetic: none -> 2.3 us  [local_run(): return (4.0 * now, 8.0 * (now - old))]
where the time goes in v3:
time: 43.3 us; the launch traced here: 43.2 us
  Pallas kernels  40.3 us (93%)
  other arithmetic  2.3 us (5%)
  between operations  0.64 us (1%)
    pallas_call x1, Pallas kernels, local_run(): pl.pallas_call(functools.partial(kernel, rows, cols, steps, kr, halo, row...  40.3 us
    mul x1, other arithmetic, local_run(): return (4.0 * now, 8.0 * (now - old))  2.3 us

profile of v3, /device:TPU:97, one launch (start us, length us, event | category | flops | bytes accessed | tf_op | source)
XLA Modules:
  0.0 43.2 jit_solution(9017003887391124016)
XLA Ops:
  0.6 40.3 %shard_map.50 = (f32[256,512]{1,0:T(8,128)}, f32[256,512]{1,0:T(8,128)}) custom-call(f32[256,512]{1,0:T(8,128)} %u_ref.1, f32[256,512]{1,0:T(8,128)} %v_ref.1, f32[3,3,64]{2,1,0:T(4,128)} %bitcast.1), custom_call_target="tpu_custom_call" | custom-call | tf_op jit(solution)/shard_map/pallas_call | solution.py:283
  40.9 2.3 %subtract_multiply_fusion = (f32[256,512]{1,0:T(8,128)}, f32[256,512]{1,0:T(8,128)}) fusion(f32[256,512]{1,0:T(8,128)} %get-tuple-element.4, f32[256,512]{1,0:T(8,128)} %get-tuple-element.5), kind=kLoop, calls=%fused_computation | loop fusion | flops 393216 | bytes 2097152 | tf_op jit(solution)/shard_map/mul | solution.py:312

commit v4 on v3

--- a/solution.py
+++ b/solution.py
@@ -11,7 +11,8 @@
 SUB = 8
 NC = 5
 UNROLL = 4
-FIRST = 10
+BLOCK = 2
+FIRST = 12
 PAD = 3 * SUB
 MESH = pl.DeviceIdType.MESH
 
@@ -49,31 +50,32 @@
     )
 
 
-def stencil_group(xs, cur, coeffs, r0):
-    w01, w10, al, be, cc = coeffs
+def stencil_rows(xs, cur, coeffs, r0):
+    tall = SUB * BLOCK
+    w01, w10, al, be, cc = (jnp.tile(w, (BLOCK, 1)) for w in coeffs)
     prv = 1 - cur
-    above = xs[cur, :, pl.ds(r0 - 1, SUB), :]
-    mid = xs[cur, :, pl.ds(r0, SUB), :]
-    below = xs[cur, :, pl.ds(r0 + 1, SUB), :]
+    above = xs[cur, :, pl.ds(r0 - 1, tall), :]
+    mid = xs[cur, :, pl.ds(r0, tall), :]
+    below = xs[cur, :, pl.ds(r0 + 1, tall), :]
     s = above + below
     q = al * s + w10 * mid
     r = be * (above - below)
     x = q + r
     y = q - r
-    z = (w01 * s + cc * mid) - xs[prv, :, pl.ds(r0, SUB), :]
+    z = (w01 * s + cc * mid) - xs[prv, :, pl.ds(r0, tall), :]
     x_wrap = pltpu.roll(x[NC - 1], 1, 1)
     y_wrap = pltpu.roll(y[0], LANES - 1, 1)
     for c in range(NC):
         xc = x[c - 1] if c else x_wrap
         yc = y[c + 1] if c < NC - 1 else y_wrap
-        xs[prv, c, pl.ds(r0, SUB), :] = (z[c] + xc) + yc
+        xs[prv, c, pl.ds(r0, tall), :] = (z[c] + xc) + yc
 
 
 def kernel(
     rows, cols, steps, kr, halo, row_n, col_n,
     u_ref, v_ref, w_hbm, now_ref, old_ref,
     w_ref, table, nu, nv, pk_l, pk_r, h_l, h_r, xs, got,
-    near, in_sem, send_sem, recv_sem, edge_send, edge_recv,
+    near, in_sem, out_sem, send_sem, recv_sem, edge_send, edge_recv,
 ):
     my_row, my_col = lax.axis_index("row"), lax.axis_index("col")
     up, down = lax.rem(my_row + row_n - 1, row_n), lax.rem(my_row + 1, row_n)
@@ -133,6 +135,14 @@
             send(n.at[pl.ds(rows, kr)], n.at[top], down, my_col)
         for r in (up, down):
             pl.semaphore_signal(near, inc=1, device_id={"row": r}, device_id_type=MESH)
+        load_w.wait()
+
+        def tabulate(t, _):
+            for k, x in enumerate(step_coeffs(w_ref, t)):
+                table[t, k] = x
+            return 0
+
+        lax.fori_loop(0, steps, tabulate, 0, unroll=4)
         pl.semaphore_wait(near, 2)
         send(pk_l.at[pl.ds(0, kr)], h_r.at[bottom], up, left)
         send(pk_l.at[pl.ds(rows - kr, kr)], h_r.at[top], down, left)
@@ -141,43 +151,66 @@
     residue = lax.rem(lane, NC)
     masks = [residue == m for m in range(NC)]
     base = PAD
-    load_w.wait()
-
-    def tabulate(t, _):
-        for k, x in enumerate(step_coeffs(w_ref, t)):
-            table[t, k] = x
-        return 0
-
-    lax.fori_loop(0, steps, tabulate, 0, unroll=4)
-    for c in sends:
+    where_to = [
+        ((NC * lane + (c - halo) % LANES) & (LANES - 1), [masks[(c - halo - LANES * b) % NC] for b in range(nblk + 1)])
+        for c in range(NC)
+    ]
+
+    def to_lanes(first, count, own_only):
+        for c, (idx, sel) in enumerate(where_to):
+            def body(g, _, c=c, idx=idx, sel=sel):
+                at = pl.ds(pl.multiple_of(first + SUB * g, SUB), SUB)
+                out = pl.ds(pl.multiple_of(base - kr + first + SUB * g, SUB), SUB)
+                ub = [nu[at, b * LANES : (b + 1) * LANES] for b in range(nblk)]
+                vb = [nv[at, b * LANES : (b + 1) * LANES] for b in range(nblk)]
+                if not own_only:
+                    ub, vb = ub + [h_l[at, :]], vb + [h_r[at, :]]
+                ul = 0.25 * permute(pick(sel[: len(ub)], ub), idx)
+                vl = permute(pick(sel[: len(vb)], vb), idx)
+                xs[0, c, out, :] = ul
+                xs[1, c, out, :] = ul - 0.125 * vl
+                return 0
+
+            lax.fori_loop(0, count // SUB, body, 0, unroll=min(count // SUB, 8))
+
+    def unpack(first, count):
+        def body(g, _):
+            at = pl.ds(pl.multiple_of(first + SUB * g, SUB), SUB)
+            hl, hr = h_l[at, :], h_r[at, :]
+            h_l[at, :] = jnp.where(low, hr, hl)
+            h_r[at, :] = pltpu.roll(jnp.where(low, hl, hr), halo, 1)
+            return 0
+
+        lax.fori_loop(0, count // SUB, body, 0, unroll=min(count // SUB, 8))
+
+    def add_halo(first, count):
+        for c, (idx, _) in enumerate(where_to):
+            column = NC * lane + c
+            outside = (column < halo) | (column >= halo + cols)
+
+            def body(g, _, c=c, idx=idx, outside=outside):
+                at = pl.ds(pl.multiple_of(first + SUB * g, SUB), SUB)
+                out = pl.ds(pl.multiple_of(base - kr + first + SUB * g, SUB), SUB)
+                ul = 0.25 * permute(h_l[at, :], idx)
+                vl = permute(h_r[at, :], idx)
+                xs[0, c, out, :] = jnp.where(outside, ul, xs[0, c, out, :])
+                xs[1, c, out, :] = jnp.where(outside, ul - 0.125 * vl, xs[1, c, out, :])
+                return 0
+
+            lax.fori_loop(0, count // SUB, body, 0, unroll=min(count // SUB, 8))
+
+    to_lanes(kr, rows, True)
+    for c in sends[:2]:
         c.wait()
-
-    def unpack(g, _):
-        at = pl.ds(pl.multiple_of(SUB * g, SUB), SUB)
-        hl, hr = h_l[at, :], h_r[at, :]
-        h_l[at, :] = jnp.where(low, hr, hl)
-        h_r[at, :] = pltpu.roll(jnp.where(low, hl, hr), halo, 1)
-        return 0
-
-    groups = (rows + 2 * kr) // SUB
-    lax.fori_loop(0, groups, unpack, 0, unroll=groups // 3)
-
-    for c in range(NC):
-        idx = (NC * lane + (c - halo) % LANES) & (LANES - 1)
-        sel = [masks[(c - halo - LANES * b) % NC] for b in range(nblk + 1)]
-
-        def to_lanes(g, _, c=c, idx=idx, sel=sel):
-            at = pl.ds(pl.multiple_of(SUB * g, SUB), SUB)
-            out = pl.ds(pl.multiple_of(base - kr + SUB * g, SUB), SUB)
-            ub = [nu[at, b * LANES : (b + 1) * LANES] for b in range(nblk)] + [h_l[at, :]]
-            vb = [nv[at, b * LANES : (b + 1) * LANES] for b in range(nblk)] + [h_r[at, :]]
-            ul = 0.25 * permute(pick(sel, ub), idx)
-            vl = permute(pick(sel, vb), idx)
-            x0[c, out, :] = ul
-            x1[c, out, :] = ul - 0.125 * vl
-            return 0
-
-        lax.fori_loop(0, groups, to_lanes, 0, unroll=groups // 3)
+    unpack(kr, half)
+    add_halo(kr, half)
+    for c in sends[2:]:
+        c.wait()
+    unpack(kr + half, half)
+    add_halo(kr + half, half)
+    for first in (0, kr + rows):
+        unpack(first, kr)
+        to_lanes(first, kr, False)
 
     TOP, BOTTOM = 0, 1
     cut = SUB * FIRST
@@ -221,8 +254,8 @@
                 t = kr * p + t0 + UNROLL * i + j
                 coeffs = [table[t, k] for k in range(5)]
                 r0 = base + start + sign * (t0 + j) + sign * UNROLL * i
-                for g in range(n):
-                    stencil_group(xs, j % 2, coeffs, r0 + SUB * g)
+                for g in range(0, n, BLOCK):
+                    stencil_rows(xs, j % 2, coeffs, r0 + SUB * g)
             return 0
 
         lax.fori_loop(0, count // UNROLL, some, 0)
@@ -257,15 +290,27 @@
 
     def to_natural(g, _):
         at = pl.ds(pl.multiple_of(base + SUB * g, SUB), SUB)
-        to = pl.ds(pl.multiple_of(SUB * g, SUB), SUB)
-        for x, out in ((x0, now_ref), (x1, old_ref)):
+        to = pl.ds(pl.multiple_of(kr + SUB * g, SUB), SUB)
+        for x, out in ((x0, nu), (x1, nv)):
             parts = [permute(x[c, at, :], idx[c]) for c in range(NC)]
             for b in range(nblk):
                 sel = [masks[(c - halo - LANES * b) % NC] for c in range(NC)]
                 out[to, b * LANES : (b + 1) * LANES] = pick(sel, parts)
         return 0
 
-    lax.fori_loop(0, rows // SUB, to_natural, 0, unroll=8)
+    stores = []
+    chunk = rows // 4
+    for k in range(4):
+        lax.fori_loop(k * chunk // SUB, (k + 1) * chunk // SUB, to_natural, 0, unroll=8)
+        for i, (x, out) in enumerate(((nu, now_ref), (nv, old_ref))):
+            stores.append(
+                pltpu.make_async_copy(
+                    x.at[pl.ds(kr + k * chunk, chunk)], out.at[pl.ds(k * chunk, chunk)], out_sem.at[i, k]
+                )
+            )
+            stores[-1].start()
+    for c in stores:
+        c.wait()
 
 
 def solution(mesh):
@@ -288,7 +333,7 @@
                 pl.BlockSpec(memory_space=pl.ANY),
                 pl.BlockSpec(memory_space=pl.ANY),
             ],
-            out_specs=(pl.BlockSpec(memory_space=pltpu.VMEM), pl.BlockSpec(memory_space=pltpu.VMEM)),
+            out_specs=(pl.BlockSpec(memory_space=pl.ANY), pl.BlockSpec(memory_space=pl.ANY)),
             scratch_shapes=[
                 pltpu.SMEM((3, 3, steps), f32),
                 pltpu.VMEM((steps, 5, SUB, LANES), f32),
@@ -302,6 +347,7 @@
                 pltpu.VMEM((2, 2, 2, NC, kr, LANES), f32),
                 pltpu.SemaphoreType.REGULAR,
                 pltpu.SemaphoreType.DMA((3,)),
+                pltpu.SemaphoreType.DMA((2, 4)),
                 pltpu.SemaphoreType.DMA((12,)),
                 pltpu.SemaphoreType.DMA((12,)),
                 pltpu.SemaphoreType.DMA((2, 2, 2)),

time: 43.3 us -> 41.4 us (0.956)
  Pallas kernels: 40.3 us -> 38.4 us
    pallas_call x1, Pallas kernels: 40.3 us -> 38.4 us  [local_run(): pl.pallas_call(functools.partial(kernel, rows, cols, steps, kr, halo, row...]
where the time goes in v4:
time: 41.4 us; the launch traced here: 41.3 us
  Pallas kernels  38.4 us (93%)
  other arithmetic  2.3 us (6%)
  between operations  0.64 us (2%)
    pallas_call x1, Pallas kernels, local_run(): pl.pallas_call(functools.partial(kernel, rows, cols, steps, kr, halo, row...  38.4 us
    mul x1, other arithmetic, local_run(): return (4.0 * now, 8.0 * (now - old))  2.3 us

profile of v4, /device:TPU:97, one launch (start us, length us, event | category | flops | bytes accessed | tf_op | source)
XLA Modules:
  0.0 41.3 jit_solution(14604102404131128821)
XLA Ops:
  0.6 38.4 %shard_map.50 = (f32[256,512]{1,0:T(8,128)}, f32[256,512]{1,0:T(8,128)}) custom-call(f32[256,512]{1,0:T(8,128)} %u_ref.1, f32[256,512]{1,0:T(8,128)} %v_ref.1, f32[3,3,64]{2,1,0:T(4,128)} %bitcast.1), custom_call_target="tpu_custom_call" | custom-call | tf_op jit(solution)/shard_map/pallas_call | solution.py:328
  39.0 2.3 %subtract_multiply_fusion = (f32[256,512]{1,0:T(8,128)}, f32[256,512]{1,0:T(8,128)}) fusion(f32[256,512]{1,0:T(8,128)} %get-tuple-element.4, f32[256,512]{1,0:T(8,128)} %get-tuple-element.5), kind=kLoop, calls=%fused_computation | loop fusion | flops 393216 | bytes 2097152 | tf_op jit(solution)/shard_map/mul | solution.py:358

commit v5 on v4

--- a/solution.py
+++ b/solution.py
@@ -10,8 +10,7 @@
 LANES = 128
 SUB = 8
 NC = 5
-UNROLL = 4
-BLOCK = 2
+PIECES = 2
 FIRST = 12
 PAD = 3 * SUB
 MESH = pl.DeviceIdType.MESH
@@ -50,9 +49,9 @@
     )
 
 
-def stencil_rows(xs, cur, coeffs, r0):
-    tall = SUB * BLOCK
-    w01, w10, al, be, cc = (jnp.tile(w, (BLOCK, 1)) for w in coeffs)
+def stencil_rows(xs, cur, coeffs, r0, block):
+    tall = SUB * block
+    w01, w10, al, be, cc = (jnp.tile(w, (block, 1)) for w in coeffs)
     prv = 1 - cur
     above = xs[cur, :, pl.ds(r0 - 1, tall), :]
     mid = xs[cur, :, pl.ds(r0, tall), :]
@@ -215,8 +214,6 @@
     TOP, BOTTOM = 0, 1
     cut = SUB * FIRST
     part = lax.rem(my_row, 2)
-    many, fewer, other = FIRST + kr // SUB, FIRST, (rows - cut + kr) // SUB
-    mid = kr // 2
     n_phase = steps // kr
 
     def edge_copies(side, slot):
@@ -248,37 +245,35 @@
             for c in edge_copies(side, lax.rem(p, 2)):
                 c.start()
 
-    def part_steps(p, t0, count, start, sign, n):
-        def some(i, _):
-            for j in range(UNROLL):
-                t = kr * p + t0 + UNROLL * i + j
-                coeffs = [table[t, k] for k in range(5)]
-                r0 = base + start + sign * (t0 + j) + sign * UNROLL * i
-                for g in range(0, n, BLOCK):
-                    stencil_rows(xs, j % 2, coeffs, r0 + SUB * g)
-            return 0
-
-        lax.fori_loop(0, count // UNROLL, some, 0)
+    def part_steps(p, first_part, sign):
+        for t in range(kr):
+            rows_needed = cut + kr - 1 - 2 * t if first_part else rows - cut + kr - 1
+            n = -(-rows_needed // SUB)
+            at_cut = cut if sign < 0 else rows - cut
+            below_cut = first_part == (sign < 0)
+            start = base + at_cut + sign * t - (SUB * n if below_cut else 0)
+            coeffs = [table[kr * p + t, k] for k in range(5)]
+            block = -(-n // PIECES)
+            for g in range(0, n, block):
+                stencil_rows(xs, t % 2, coeffs, start + SUB * g, min(block, n - g))
 
     def phase(p, _):
         @pl.when(part == 0)
         def _():
             take_halo(TOP, p)
-            part_steps(p, 0, mid, cut - SUB * many, -1, many)
-            part_steps(p, mid, kr - mid, cut - SUB * fewer, -1, fewer)
+            part_steps(p, True, -1)
             send_edge(TOP, p)
             take_halo(BOTTOM, p)
-            part_steps(p, 0, kr, cut, -1, other)
+            part_steps(p, False, -1)
             send_edge(BOTTOM, p)
 
         @pl.when(part == 1)
         def _():
             take_halo(BOTTOM, p)
-            part_steps(p, 0, mid, rows - cut, 1, many)
-            part_steps(p, mid, kr - mid, rows - cut, 1, fewer)
+            part_steps(p, True, 1)
             send_edge(BOTTOM, p)
             take_halo(TOP, p)
-            part_steps(p, 0, kr, rows - cut - SUB * other, 1, other)
+            part_steps(p, False, 1)
             send_edge(TOP, p)
 
         return 0

time: 41.4 us -> 40.2 us (0.971)
  Pallas kernels: 38.4 us -> 37.1 us
    pallas_call x1, Pallas kernels: 38.4 us -> 37.1 us  [local_run(): pl.pallas_call(functools.partial(kernel, rows, cols, steps, kr, halo, row...]
where the time goes in v5:
time: 40.2 us; the launch traced here: 40 us
  Pallas kernels  37.1 us (92%)
  other arithmetic  2.3 us (6%)
  between operations  0.64 us (2%)
    pallas_call x1, Pallas kernels, local_run(): pl.pallas_call(functools.partial(kernel, rows, cols, steps, kr, halo, row...  37.1 us
    mul x1, other arithmetic, local_run(): return (4.0 * now, 8.0 * (now - old))  2.3 us

profile of v5, /device:TPU:97, one launch (start us, length us, event | category | flops | bytes accessed | tf_op | source)
XLA Modules:
  0.0 40.0 jit_solution(979625389382963911)
XLA Ops:
  0.6 37.1 %shard_map.50 = (f32[256,512]{1,0:T(8,128)}, f32[256,512]{1,0:T(8,128)}) custom-call(f32[256,512]{1,0:T(8,128)} %u_ref.1, f32[256,512]{1,0:T(8,128)} %v_ref.1, f32[3,3,64]{2,1,0:T(4,128)} %bitcast.1), custom_call_target="tpu_custom_call" | custom-call | tf_op jit(solution)/shard_map/pallas_call | solution.py:323
  37.7 2.3 %subtract_multiply_fusion = (f32[256,512]{1,0:T(8,128)}, f32[256,512]{1,0:T(8,128)}) fusion(f32[256,512]{1,0:T(8,128)} %get-tuple-element.4, f32[256,512]{1,0:T(8,128)} %get-tuple-element.5), kind=kLoop, calls=%fused_computation | loop fusion | flops 393216 | bytes 2097152 | tf_op jit(solution)/shard_map/mul | solution.py:353

commit v6 on v5

--- a/solution.py
+++ b/solution.py
@@ -14,6 +14,10 @@
 FIRST = 12
 PAD = 3 * SUB
 MESH = pl.DeviceIdType.MESH
+
+
+def unroll_of(n):
+    return max(k for k in range(1, 10) if n % k == 0)
 
 
 def lane_iota():
@@ -109,6 +113,8 @@
 
     lax.fori_loop(0, rows // SUB, pack, 0, unroll=8)
     pl.semaphore_wait(barrier, len(around))
+    for r in (up, down):
+        pl.semaphore_signal(near, inc=1, device_id={"row": r}, device_id_type=MESH)
     sends = []
 
     def send(src, dst, r, c):
@@ -121,32 +127,42 @@
         sends.append(copy)
 
     top, bottom = pl.ds(0, kr), pl.ds(kr + rows, kr)
-    half = rows // 2
-    for first in (0, half):
-        at = pl.ds(first, half)
-        to = pl.ds(kr + first, half)
+    TOP, BOTTOM = 0, 1
+    part = lax.rem(my_row, 2)
+    cut = SUB * FIRST
+    early_rows = cut + kr
+    late_rows = rows - early_rows
+    early_at, late_at = part * late_rows, (1 - part) * early_rows
+    landing = {TOP: [], BOTTOM: []}
+
+    def send_columns(first, count):
+        at = pl.ds(pl.multiple_of(first, SUB), count)
+        to = pl.ds(pl.multiple_of(kr + first, SUB), count)
         send(pk_l.at[at], h_r.at[to], my_row, left)
         send(pk_r.at[at], h_l.at[to], my_row, right)
-        if first:
-            break
-        for n in (nu, nv):
-            send(n.at[pl.ds(kr, kr)], n.at[bottom], up, my_col)
-            send(n.at[pl.ds(rows, kr)], n.at[top], down, my_col)
-        for r in (up, down):
-            pl.semaphore_signal(near, inc=1, device_id={"row": r}, device_id_type=MESH)
-        load_w.wait()
-
-        def tabulate(t, _):
-            for k, x in enumerate(step_coeffs(w_ref, t)):
-                table[t, k] = x
-            return 0
-
-        lax.fori_loop(0, steps, tabulate, 0, unroll=4)
-        pl.semaphore_wait(near, 2)
-        send(pk_l.at[pl.ds(0, kr)], h_r.at[bottom], up, left)
-        send(pk_l.at[pl.ds(rows - kr, kr)], h_r.at[top], down, left)
-        send(pk_r.at[pl.ds(0, kr)], h_l.at[bottom], up, right)
-        send(pk_r.at[pl.ds(rows - kr, kr)], h_l.at[top], down, right)
+        return sends[-2:]
+
+    early = send_columns(early_at, early_rows)
+    for n in (nu, nv):
+        send(n.at[pl.ds(kr, kr)], n.at[bottom], up, my_col)
+        landing[BOTTOM].append(sends[-1])
+        send(n.at[pl.ds(rows, kr)], n.at[top], down, my_col)
+        landing[TOP].append(sends[-1])
+    load_w.wait()
+
+    def tabulate(t, _):
+        for k, x in enumerate(step_coeffs(w_ref, t)):
+            table[t, k] = x
+        return 0
+
+    lax.fori_loop(0, steps, tabulate, 0, unroll=4)
+    pl.semaphore_wait(near, 2)
+    for pk, h, c in ((pk_l, h_r, left), (pk_r, h_l, right)):
+        send(pk.at[pl.ds(0, kr)], h.at[bottom], up, c)
+        landing[BOTTOM].append(sends[-1])
+        send(pk.at[pl.ds(rows - kr, kr)], h.at[top], down, c)
+        landing[TOP].append(sends[-1])
+    late = send_columns(late_at, late_rows)
     residue = lax.rem(lane, NC)
     masks = [residue == m for m in range(NC)]
     base = PAD
@@ -170,7 +186,7 @@
                 xs[1, c, out, :] = ul - 0.125 * vl
                 return 0
 
-            lax.fori_loop(0, count // SUB, body, 0, unroll=min(count // SUB, 8))
+            lax.fori_loop(0, count // SUB, body, 0, unroll=unroll_of(count // SUB))
 
     def unpack(first, count):
         def body(g, _):
@@ -180,7 +196,7 @@
             h_r[at, :] = pltpu.roll(jnp.where(low, hl, hr), halo, 1)
             return 0
 
-        lax.fori_loop(0, count // SUB, body, 0, unroll=min(count // SUB, 8))
+        lax.fori_loop(0, count // SUB, body, 0, unroll=unroll_of(count // SUB))
 
     def add_halo(first, count):
         for c, (idx, _) in enumerate(where_to):
@@ -196,24 +212,26 @@
                 xs[1, c, out, :] = jnp.where(outside, ul - 0.125 * vl, xs[1, c, out, :])
                 return 0
 
-            lax.fori_loop(0, count // SUB, body, 0, unroll=min(count // SUB, 8))
-
-    to_lanes(kr, rows, True)
-    for c in sends[:2]:
-        c.wait()
-    unpack(kr, half)
-    add_halo(kr, half)
-    for c in sends[2:]:
-        c.wait()
-    unpack(kr + half, half)
-    add_halo(kr + half, half)
-    for first in (0, kr + rows):
+            lax.fori_loop(0, count // SUB, body, 0, unroll=unroll_of(count // SUB))
+
+    def take_columns(copies, first, count):
+        for c in copies:
+            c.wait()
+        unpack(kr + first, count)
+        add_halo(kr + first, count)
+
+    def take_rows(side):
+        for c in landing[side]:
+            c.wait()
+        first = (0, kr + rows)[side]
         unpack(first, kr)
         to_lanes(first, kr, False)
 
-    TOP, BOTTOM = 0, 1
-    cut = SUB * FIRST
-    part = lax.rem(my_row, 2)
+    to_lanes(kr, rows, True)
+    take_columns(early, early_at, early_rows)
+    for side in (TOP, BOTTOM):
+        pl.when(part == side)(functools.partial(take_rows, side))
+
     n_phase = steps // kr
 
     def edge_copies(side, slot):
@@ -257,12 +275,19 @@
             for g in range(0, n, block):
                 stencil_rows(xs, t % 2, coeffs, start + SUB * g, min(block, n - g))
 
+    def take_late(side, p):
+        @pl.when(p == 0)
+        def _():
+            take_columns(late, (early_rows, 0)[1 - side], late_rows)
+            take_rows(side)
+
     def phase(p, _):
         @pl.when(part == 0)
         def _():
             take_halo(TOP, p)
             part_steps(p, True, -1)
             send_edge(TOP, p)
+            take_late(BOTTOM, p)
             take_halo(BOTTOM, p)
             part_steps(p, False, -1)
             send_edge(BOTTOM, p)
@@ -272,6 +297,7 @@
             take_halo(BOTTOM, p)
             part_steps(p, True, 1)
             send_edge(BOTTOM, p)
+            take_late(TOP, p)
             take_halo(TOP, p)
             part_steps(p, False, 1)
             send_edge(TOP, p)
@@ -283,20 +309,27 @@
     inv = pow(NC, -1, LANES)
     idx = [(inv * (lane + (halo - c) % LANES)) & (LANES - 1) for c in range(NC)]
 
+    wide = 4
     def to_natural(g, _):
-        at = pl.ds(pl.multiple_of(base + SUB * g, SUB), SUB)
-        to = pl.ds(pl.multiple_of(kr + SUB * g, SUB), SUB)
-        for x, out in ((x0, nu), (x1, nv)):
-            parts = [permute(x[c, at, :], idx[c]) for c in range(NC)]
-            for b in range(nblk):
-                sel = [masks[(c - halo - LANES * b) % NC] for c in range(NC)]
-                out[to, b * LANES : (b + 1) * LANES] = pick(sel, parts)
+        ats = [pl.multiple_of(SUB * (wide * g + k), SUB) for k in range(wide)]
+        parts = {}
+        for c in range(NC):
+            for k in range(wide):
+                for i in range(2):
+                    parts[i, k, c] = permute(xs[i, c, pl.ds(base + ats[k], SUB), :], idx[c])
+        for k in range(wide):
+            for i, out in enumerate((nu, nv)):
+                for b in range(nblk):
+                    sel = [masks[(c - halo - LANES * b) % NC] for c in range(NC)]
+                    out[pl.ds(kr + ats[k], SUB), b * LANES : (b + 1) * LANES] = pick(
+                        sel, [parts[i, k, c] for c in range(NC)]
+                    )
         return 0
 
     stores = []
     chunk = rows // 4
     for k in range(4):
-        lax.fori_loop(k * chunk // SUB, (k + 1) * chunk // SUB, to_natural, 0, unroll=8)
+        lax.fori_loop(k * chunk // (SUB * wide), (k + 1) * chunk // (SUB * wide), to_natural, 0, unroll=2)
         for i, (x, out) in enumerate(((nu, now_ref), (nv, old_ref))):
             stores.append(
                 pltpu.make_async_copy(

time: 40.2 us -> 39.6 us (0.985)
  Pallas kernels: 37.1 us -> 36.5 us
    pallas_call x1, Pallas kernels: 37.1 us -> 36.5 us  [local_run(): pl.pallas_call(functools.partial(kernel, rows, cols, steps, kr, halo, row...]
where the time goes in v6:
time: 39.6 us; the launch traced here: 39.5 us
  Pallas kernels  36.5 us (92%)
  other arithmetic  2.3 us (6%)
  between operations  0.64 us (2%)
    pallas_call x1, Pallas kernels, local_run(): pl.pallas_call(functools.partial(kernel, rows, cols, steps, kr, halo, row...  36.5 us
    mul x1, other arithmetic, local_run(): return (4.0 * now, 8.0 * (now - old))  2.3 us

profile of v6, /device:TPU:97, one launch (start us, length us, event | category | flops | bytes accessed | tf_op | source)
XLA Modules:
  0.0 39.5 jit_solution(3209544535452988250)
XLA Ops:
  0.6 36.5 %shard_map.50 = (f32[256,512]{1,0:T(8,128)}, f32[256,512]{1,0:T(8,128)}) custom-call(f32[256,512]{1,0:T(8,128)} %u_ref.1, f32[256,512]{1,0:T(8,128)} %v_ref.1, f32[3,3,64]{2,1,0:T(4,128)} %bitcast.1), custom_call_target="tpu_custom_call" | custom-call | tf_op jit(solution)/shard_map/pallas_call | solution.py:356
  37.2 2.3 %subtract_multiply_fusion = (f32[256,512]{1,0:T(8,128)}, f32[256,512]{1,0:T(8,128)}) fusion(f32[256,512]{1,0:T(8,128)} %get-tuple-element.4, f32[256,512]{1,0:T(8,128)} %get-tuple-element.5), kind=kLoop, calls=%fused_computation | loop fusion | flops 393216 | bytes 2097152 | tf_op jit(solution)/shard_map/mul | solution.py:386

commit v7 on v6

--- a/solution.py
+++ b/solution.py
@@ -143,11 +143,6 @@
         return sends[-2:]
 
     early = send_columns(early_at, early_rows)
-    for n in (nu, nv):
-        send(n.at[pl.ds(kr, kr)], n.at[bottom], up, my_col)
-        landing[BOTTOM].append(sends[-1])
-        send(n.at[pl.ds(rows, kr)], n.at[top], down, my_col)
-        landing[TOP].append(sends[-1])
     load_w.wait()
 
     def tabulate(t, _):
@@ -161,6 +156,11 @@
         send(pk.at[pl.ds(0, kr)], h.at[bottom], up, c)
         landing[BOTTOM].append(sends[-1])
         send(pk.at[pl.ds(rows - kr, kr)], h.at[top], down, c)
+        landing[TOP].append(sends[-1])
+    for n in (nu, nv):
+        send(n.at[pl.ds(kr, kr)], n.at[bottom], up, my_col)
+        landing[BOTTOM].append(sends[-1])
+        send(n.at[pl.ds(rows, kr)], n.at[top], down, my_col)
         landing[TOP].append(sends[-1])
     late = send_columns(late_at, late_rows)
     residue = lax.rem(lane, NC)

time: 39.6 us -> 39.6 us (level)
  no operation moved by 1% of the time
where the time goes in v7:
time: 39.6 us; the launch traced here: 39.5 us
  Pallas kernels  36.5 us (92%)
  other arithmetic  2.3 us (6%)
  between operations  0.64 us (2%)
    pallas_call x1, Pallas kernels, local_run(): pl.pallas_call(functools.partial(kernel, rows, cols, steps, kr, halo, row...  36.5 us
    mul x1, other arithmetic, local_run(): return (4.0 * now, 8.0 * (now - old))  2.3 us

profile of v7, /device:TPU:97, one launch (start us, length us, event | category | flops | bytes accessed | tf_op | source)
XLA Modules:
  0.0 39.5 jit_solution(1250629226839983572)
XLA Ops:
  0.6 36.5 %shard_map.50 = (f32[256,512]{1,0:T(8,128)}, f32[256,512]{1,0:T(8,128)}) custom-call(f32[256,512]{1,0:T(8,128)} %u_ref.1, f32[256,512]{1,0:T(8,128)} %v_ref.1, f32[3,3,64]{2,1,0:T(4,128)} %bitcast.1), custom_call_target="tpu_custom_call" | custom-call | tf_op jit(solution)/shard_map/pallas_call | solution.py:356
  37.2 2.3 %subtract_multiply_fusion = (f32[256,512]{1,0:T(8,128)}, f32[256,512]{1,0:T(8,128)}) fusion(f32[256,512]{1,0:T(8,128)} %get-tuple-element.4, f32[256,512]{1,0:T(8,128)} %get-tuple-element.5), kind=kLoop, calls=%fused_computation | loop fusion | flops 393216 | bytes 2097152 | tf_op jit(solution)/shard_map/mul | solution.py:386
